TPU v7x, 32 devices: a whole 2x2x4 slice. The times are simulated.
32 devices in a mesh: bank: 8 (over y, x, core), zero: 4 (over z).
Axes of the slice: x: 2, y: 2, z: 4, core: 2. Of those that a mesh axis runs over, the one named last changes fastest.
Arguments:
- master_down: float32 [64, 1024, 2048], P('bank', None, 'zero'), may hold values from -0.25 to 0.25
- router_weight: float32 [2048, 64], P('zero', 'bank'), may hold values from -0.125 to 0.125
- router_gain: float32 [2048], P('zero'), may hold values from 0.25 to 1.75
Outputs:
- final_down: bfloat16 [64, 1024, 2048], P('bank')
- scale_down: float32 [64, 1024], P('bank')
- serve_router: bfloat16 [2048, 64], replicated
All inputs are finite; a program needn't handle non-finite values. Where the computation divides by a largest or mean magnitude, that divisor is 1e-20 or more.
Results may differ from a plain program's by a relative error of at most 0.001.
Values may be sent and summed in bfloat16 or wider, within the bound.
A program may use at most 128 MiB of HBM per device.

v0:
```python
import jax
import jax.numpy as jnp
from jax import lax
from jax.sharding import PartitionSpec as P


def per_device(master_down, router_weight, router_gain):
    scale_down = lax.pmax(jnp.max(jnp.abs(master_down), axis=2), "zero")
    narrow_down = (master_down / jnp.expand_dims(scale_down, 2)).astype(jnp.bfloat16)
    final_down = lax.all_gather(narrow_down, "zero", axis=2, tiled=True)
    part_router = (router_weight * router_gain[:, None]).astype(jnp.bfloat16)
    row_router = lax.all_gather(part_router, "zero", axis=0, tiled=True)
    serve_router = lax.all_gather(row_router, "bank", axis=1, tiled=True)
    return (final_down, scale_down, serve_router)


def solution(mesh):
    placed = (P("bank", None, "zero"), P("zero", "bank"), P("zero"))
    return jax.shard_map(
        per_device,
        mesh=mesh,
        in_specs=placed,
        out_specs=(P("bank", None, None), P("bank", None), P()),
        check_vma=False,
    )
```

profile of v0, /device:TPU:0, one launch (start us, length us, event | category | flops | bytes accessed | tf_op | source)
XLA Modules:
  0.0 634.6 jit_solution(17249483322936477532)
XLA Ops:
  7.2 0.0 all-gather.2.cloned.1.call-start
  7.2 7.1 %abs_reduce_fusion = f32[8,1024]{1,0:T(8,128)S(1)} fusion(f32[8,1024,512]{2,1,0:T(8,128)} %param.3), kind=kLoop, calls=%fused_computation.1 | loop fusion | flops 8380416 | bytes 16809984 | tf_op jit(solution)/shard_map/reduce_max | solution.py:8
  14.3 20.8 %pmax.7 = f32[8,1024]{1,0:T(8,128)S(1)} all-reduce(f32[8,1024]{1,0:T(8,128)S(1)} %abs_reduce_fusion), channel_id=1, replica_groups=mesh['bank'=8,'zero'=4] {'zero'}, use_global_device_ids=true, to_apply=%region_1.0 | all-reduce | flops 8192 | bytes 65536 | tf_op jit(solution)/shard_map/pmax | solution.py:8
  35.1 0.0 copy-start
  35.1 0.0 copy-start.1
  35.2 0.0 copy-start.2
  35.2 9.2 %divide_convert_fusion = bf16[8,1024,512]{2,1,0:T(8,128)(2,1)} fusion(f32[8,1024,512]{2,1,0:T(8,128)} %param.3, f32[8,1024]{1,0:T(8,128)S(1)} %pmax.7), kind=kLoop, calls=%fused_computation | loop fusion | flops 8388608 | bytes 25198592 | tf_op jit(solution)/shard_map/convert_element_type | solution.py:9
  44.3 0.0 all-gather.2.cloned.1.call-update
  44.4 0.0 copy-done
  44.4 0.0 copy-done.1
  44.4 0.0 copy-done.2
  44.4 13.1 %all_gather.10 = bf16[2048,8]{0,1:T(8,128)(2,1)S(1)} all-gather(bf16[512,8]{0,1:T(8,128)(2,1)S(1)} %multiply_convert_fusion), channel_id=1, replica_groups=mesh['bank'=8,'zero'=4] {'zero'}, dimensions={0}, use_global_device_ids=true | all-gather | bytes 40960 | tf_op jit(solution)/shard_map/all_gather | solution.py:12
  57.5 9.3 %all_gather.11 = bf16[2048,64]{0,1:T(8,128)(2,1)S(1)} all-gather(bf16[2048,8]{0,1:T(8,128)(2,1)S(1)} %all_gather.10), channel_id=1, replica_groups=mesh['bank'=8,'zero'=4] {'bank'}, dimensions={1}, use_global_device_ids=true | all-gather | bytes 294912 | tf_op jit(solution)/shard_map/all_gather | solution.py:13
  66.8 537.3 %all-gather.2.cloned.1.call-done = bf16[8,1024,2048]{2,1,0:T(8,128)(2,1)} async-done(((bf16[8,1024,512]{2,1,0:T(8,128)(2,1)}), bf16[8,1024,2048]{2,1,0:T(8,128)(2,1)}) %all-gather.2.cloned.1.call-update) | async-done | bytes 33554448 | tf_op jit(solution)/shard_map/all_gather | solution.py:10
  604.1 22.9 %copy.8 = bf16[8,1024,2048]{2,1,0:T(8,128)(2,1)} copy(bf16[8,1024,2048]{2,1,0:T(8,128)(2,1)} %all-gather.2.cloned.1.call-done) | data formatting | bytes 67108864
  627.0 0.7 copy.9
  (1 shorter events, 0.0 us)
Async XLA Ops:
  7.2 597.0 %all-gather.2.cloned.1.call-start = ((), (), s32[]{:S(2)}) async-start(), calls=%async_computation | async-start | bytes 41943040 | tf_op jit(solution)/shard_map/all_gather | solution.py:10
  35.1 9.2 %copy-start = (f32[8,1024]{1,0:T(8,128)}, f32[8,1024]{1,0:T(8,128)S(1)}, u32[]{:S(2)}) copy-start(f32[8,1024]{1,0:T(8,128)S(1)} %pmax.7) | copy-start | bytes 98308
  35.1 9.2 %copy-start.1 = (f32[512,8]{0,1:T(8,128)S(1)}, f32[512,8]{0,1:T(8,128)}, u32[]{:S(2)}) copy-start(f32[512,8]{0,1:T(8,128)} %param.4) | copy-start | bytes 49156
  35.2 9.2 %copy-start.2 = (f32[512]{0:T(512)S(1)}, f32[512]{0:T(512)}, u32[]{:S(2)}) copy-start(f32[512]{0:T(512)} %param.5) | copy-start | bytes 6148
Sparse Core Ops, SparseCore 0:
  44.5 559.6 all-gather.1
where the time goes:
time: 635 us
  waiting for transfers between devices  537 us (85%)
  blocking collectives  43.2 us (7%)
  local copies, waits for them, and re-layouts  23.6 us (4%)
  other arithmetic  16.3 us (3%)
  between operations  14.1 us (2%)
    all_gather x1, waiting for transfers between devices, per_device(): final_down = lax.all_gather(narrow_down, 'zero', axis=2, tiled=True)  537 us
    unnamed x8, local copies, waits for them, and re-layouts  23.6 us
    pmax x1, blocking collectives, per_device(): scale_down = lax.pmax(jnp.max(jnp.abs(master_down), axis=2), 'zero')  20.8 us
    all_gather x1, blocking collectives, per_device(): row_router = lax.all_gather(part_router, 'zero', axis=0, tiled=True)  13.1 us
  transfers between devices with their start and end apart: 1, of which 1 were waited for; matrix products, arithmetic and copies ran while one was open for 0% of the time, Pallas kernels for 0%

commit v1 on v0

v1 whole, which is shorter than its diff:
```python
import functools

import jax
import jax.numpy as jnp
from jax import lax
from jax.experimental import pallas as pl
from jax.experimental.pallas import tpu as pltpu
from jax.sharding import PartitionSpec as P

MESH = pl.DeviceIdType.MESH
LANES = 128
CHUNK = 512


def remote(src, dst, send, recv, axis, peer):
    return pltpu.make_async_remote_copy(
        src_ref=src, dst_ref=dst, send_sem=send, recv_sem=recv,
        device_id={axis: peer}, device_id_type=MESH,
    )


def gather_kernel(
    n, banks, m_ref, r_ref, t_ref, s_ref, g_out,
    x, nar, mx, g, in_sem, own_sem, ls, lr, rs, rr, ms, mr, zs, zr, bs, br,
):
    z, b = lax.axis_index("zero"), lax.axis_index("bank")
    rows, w = x.shape
    experts, groups = mx.shape[1:3]
    depth = groups * LANES
    chunks = rows // CHUNK
    per = depth // CHUNK

    def load(e):
        span = pl.ds(e * depth, depth)
        return pltpu.make_async_copy(m_ref.at[span], x.at[span], in_sem.at[e])

    def maxima(e):
        load(e).wait()

        def piece(i, _):
            base = e * depth + i * LANES
            top = jnp.abs(x[pl.ds(base, LANES), 0:LANES])
            for k in range(1, w // LANES):
                top = jnp.maximum(top, jnp.abs(x[pl.ds(base, LANES), k * LANES:(k + 1) * LANES]))
            mx[z, e, pl.ds(i, 1), :] = jnp.max(top.T, axis=0, keepdims=True)
            return 0

        lax.fori_loop(0, groups, piece, 0)

    def exchange(which, first, last):
        span = pl.ds(first, last - first)
        return [
            remote(mx.at[z, span], mx.at[z, span], ms.at[which, k - 1], mr.at[which, k - 1], "zero", lax.rem(z + k, n))
            for k in range(1, n)
        ]

    def narrow(c):
        def piece(j, _):
            row = c * CHUNK + j * LANES
            e, i = row // depth, (row % depth) // LANES
            s = mx[0, e, pl.ds(i, 1), :]
            for k in range(1, n):
                s = jnp.maximum(s, mx[k, e, pl.ds(i, 1), :])
            s_ref[e, pl.ds(i, 1), :] = s
            wide = jnp.broadcast_to(s, (LANES, LANES)).T
            for k in range(w // LANES):
                part = x[pl.ds(row, LANES), k * LANES:(k + 1) * LANES] / wide
                nar[pl.ds(row, LANES), k * LANES:(k + 1) * LANES] = part.astype(nar.dtype)
            return 0

        lax.fori_loop(0, CHUNK // LANES, piece, 0)

    def span_of(c):
        return pl.ds(pl.multiple_of(c * CHUNK, CHUNK), CHUNK)

    def place(c, o):
        return t_ref.at[span_of(c), pl.ds(pl.multiple_of(o * w, LANES), w)]

    def leftward(p, c):
        src = nar.at[span_of(c)] if p == 0 else place(c, z + p)
        return remote(src, place(c, z + p), ls.at[p, c], lr.at[p, c], "zero", z - 1)

    def rightward(p, c):
        src = nar.at[span_of(c)] if p == 0 else place(c, z - p)
        return remote(src, place(c, z - p), rs.at[p, c], rr.at[p, c], "zero", z + 1)

    def from_right(p, c):
        there = place(c, z + 1 + p)
        return remote(there, there, ls.at[p, c], lr.at[p, c], "zero", z + 1)

    def from_left(p, c):
        there = place(c, z - 1 - p)
        return remote(there, there, rs.at[p, c], rr.at[p, c], "zero", z - 1)

    def own(c):
        return pltpu.make_async_copy(nar.at[span_of(c)], place(c, z), own_sem.at[c])

    def send(c):
        @pl.when(z > 0)
        def _():
            leftward(0, c).start()

        @pl.when(z < n - 1)
        def _():
            rightward(0, c).start()

        own(c).start()

    def each(first, last, body):
        def step(c, _):
            body(c)
            return 0

        lax.fori_loop(first, last, step, 0)

    each(0, experts, lambda e: load(e).start())
    barrier = pltpu.get_barrier_semaphore()
    for k in range(1, n):
        pl.semaphore_signal(barrier, inc=1, device_id={"zero": lax.rem(z + k, n)}, device_id_type=MESH)
    for k in range(1, banks):
        pl.semaphore_signal(barrier, inc=1, device_id={"bank": lax.rem(b + k, banks)}, device_id_type=MESH)
    maxima(0)
    g[b, z] = r_ref[...]
    pl.semaphore_wait(barrier, n + banks - 2)

    early = exchange(0, 0, 1)
    for copy in early:
        copy.start()
    routes = [
        remote(g.at[b, z], g.at[b, z], zs.at[k - 1], zr.at[k - 1], "zero", lax.rem(z + k, n)) for k in range(1, n)
    ]
    for copy in routes:
        copy.start()
    if experts > 1:
        maxima(1)
    for copy in early:
        copy.wait_recv()
    each(0, per, narrow)
    each(0, per, send)
    late = []
    if experts > 1:
        each(2, experts, maxima)
        late = exchange(1, 1, experts)
        for copy in late:
            copy.start()
        for copy in late:
            copy.wait_recv()
        narrow(per)

        def follow(c):
            narrow(c)
            send(c - 1)

        each(per + 1, chunks, follow)
    for copy in routes:
        copy.wait_recv()
    if experts > 1:
        send(chunks - 1)
    spread = [
        remote(g.at[b], g.at[b], bs.at[k - 1], br.at[k - 1], "bank", lax.rem(b + k, banks)) for k in range(1, banks)
    ]
    for copy in spread:
        copy.start()

    for p in range(1, n):
        def relay(c):
            @pl.when(z + p <= n - 1)
            def _():
                from_right(p - 1, c).wait_recv()

            if p < n - 1:
                @pl.when((z > 0) & (z + p <= n - 1))
                def _():
                    leftward(p, c).start()

            @pl.when(z - p >= 0)
            def _():
                from_left(p - 1, c).wait_recv()

            if p < n - 1:
                @pl.when((z < n - 1) & (z - p >= 0))
                def _():
                    rightward(p, c).start()

        each(0, chunks, relay)

    for copy in spread:
        copy.wait_recv()
    g_out[...] = g[...]
    for copy in early + late + routes + spread:
        copy.wait_send()
    each(0, chunks, lambda c: own(c).wait())
    for p in range(n - 1):
        @pl.when((z > 0) & (z + p <= n - 1))
        def _():
            each(0, chunks, lambda c: leftward(p, c).wait_send())

        @pl.when((z < n - 1) & (z - p >= 0))
        def _():
            each(0, chunks, lambda c: rightward(p, c).wait_send())


def per_device(n, banks, master_down, router_weight, router_gain):
    experts, depth, w = master_down.shape
    part, few = router_weight.shape
    rows = experts * depth
    chunks = rows // CHUNK
    groups = depth // LANES
    part_router = (router_weight * router_gain[:, None]).astype(jnp.bfloat16).T
    dma = pltpu.SemaphoreType.DMA
    gathered, scale, routed = pl.pallas_call(
        functools.partial(gather_kernel, n, banks),
        out_shape=(
            jax.ShapeDtypeStruct((rows, n * w), jnp.bfloat16),
            jax.ShapeDtypeStruct((experts, groups, LANES), jnp.float32),
            jax.ShapeDtypeStruct((banks, n, few, part), jnp.bfloat16),
        ),
        in_specs=[pl.BlockSpec(memory_space=pl.ANY), pl.BlockSpec(memory_space=pltpu.VMEM)],
        out_specs=(
            pl.BlockSpec(memory_space=pl.ANY),
            pl.BlockSpec(memory_space=pltpu.VMEM),
            pl.BlockSpec(memory_space=pltpu.VMEM),
        ),
        scratch_shapes=[
            pltpu.VMEM((rows, w), jnp.float32),
            pltpu.VMEM((rows, w), jnp.bfloat16),
            pltpu.VMEM((n, experts, groups, LANES), jnp.float32),
            pltpu.VMEM((banks, n, few, part), jnp.bfloat16),
            dma((experts,)),
            dma((chunks,)),
            dma((n - 1, chunks)),
            dma((n - 1, chunks)),
            dma((n - 1, chunks)),
            dma((n - 1, chunks)),
            dma((2, n - 1)),
            dma((2, n - 1)),
            dma((n - 1,)),
            dma((n - 1,)),
            dma((banks - 1,)),
            dma((banks - 1,)),
        ],
        compiler_params=pltpu.CompilerParams(collective_id=0, has_side_effects=True),
        name="gather",
    )(master_down.reshape(rows, w), part_router)
    serve_router = routed.transpose(1, 3, 0, 2).reshape(n * part, banks * few)
    return (
        gathered.reshape(experts, depth, n * w),
        scale.reshape(experts, depth),
        serve_router,
    )


def solution(mesh):
    placed = (P("bank", None, "zero"), P("zero", "bank"), P("zero"))
    return jax.shard_map(
        functools.partial(per_device, mesh.shape["zero"], mesh.shape["bank"]),
        mesh=mesh,
        in_specs=placed,
        out_specs=(P("bank", None, None), P("bank", None), P()),
        check_vma=False,
    )
```

time: 635 us -> 585 us (0.921)
  Pallas kernels: 0 us -> 558 us
  waiting for transfers between devices: 537 us -> 0 us
  blocking collectives: 43.2 us -> 0 us
  other arithmetic: 16.3 us -> 1.32 us
  between operations: 14.1 us -> 0.64 us
    pallas_call x0 -> x1, Pallas kernels: none -> 558 us  [per_device(): pl.pallas_call(functools.partial(gather_kernel, n, banks), out_shape=(jax...]
    all_gather x1 -> x0, waiting for transfers between devices: 537 us -> none  [per_device(): final_down = lax.all_gather(narrow_down, 'zero', axis=2, tiled=True)]
    all_gather x2 -> x0, blocking collectives: 22.4 us -> none  [the longest x1 13.1 us: per_device(): row_router = lax.all_gather(part_router, 'zero', axis=0, tiled=True)]
    pmax x1 -> x0, blocking collectives: 20.8 us -> none  [per_device(): scale_down = lax.pmax(jnp.max(jnp.abs(master_down), axis=2), 'zero')]
    convert_element_type x2 -> x0, other arithmetic: 9.18 us -> none  [the longest x1 9.17 us: per_device(): (master_down / jnp.expand_dims(scale_down, 2)).astype(jnp.bfloat16)]
    reduce_max x1 -> x0, other arithmetic: 7.09 us -> none  [per_device(): scale_down = lax.pmax(jnp.max(jnp.abs(master_down), axis=2), 'zero')]
    unnamed x8 -> x5, local copies, waits for them, and re-layouts: 23.6 us -> 25 us
  transfers between devices with their start and end apart: 1 -> 0, of which waited for: 1 -> 0; matrix products, arithmetic and copies ran while one was open for 0% -> 0% of each run, Pallas kernels for 0% -> 0%
where the time goes in v1:
time: 585 us
  Pallas kernels  558 us (95%)
  local copies, waits for them, and re-layouts  25 us (4%)
    pallas_call x1, Pallas kernels, per_device(): pl.pallas_call(functools.partial(gather_kernel, n, banks), out_shape=(jax...  558 us
    unnamed x5, local copies, waits for them, and re-layouts  25 us

profile of v1, /device:TPU:0, one launch (start us, length us, event | category | flops | bytes accessed | tf_op | source)
XLA Modules:
  0.0 584.7 jit_solution(7703411446610128330)
XLA Ops:
  0.6 1.3 fusion.r_ref
  2.0 557.7 %gather.1 = (bf16[8192,2048]{1,0:T(8,128)(2,1)}, f32[8,8,128]{2,1,0:T(8,128)}, bf16[8,4,8,512]{3,2,1,0:T(8,128)(2,1)}) custom-call(f32[8192,512]{1,0:T(8,128)} %bitcast.12, bf16[8,512]{1,0:T(8,128)(2,1)} %fusion.r_ref), custom_call_target="tpu_custom_call" | custom-call | tf_op jit(solution)/shard_map/gather/pallas_call | solution.py:211
  559.7 1.4 copy.8
  561.0 0.0 copy-start
  561.1 22.9 %copy.11 = bf16[8,1024,2048]{2,1,0:T(8,128)(2,1)} copy(bf16[8,1024,2048]{2,1,0:T(8,128)(2,1)} %bitcast.11) | data formatting | bytes 67108864
  584.0 0.0 copy-done
  584.0 0.7 copy.12
Async XLA Ops:
  561.0 22.9 %copy-start = (bf16[8,4,8,512]{3,2,1,0:T(8,128)(2,1)S(1)}, bf16[8,4,8,512]{3,2,1,0:T(8,128)(2,1)}, u32[]{:S(2)}) copy-start(bf16[8,4,8,512]{3,2,1,0:T(8,128)(2,1)} %get-tuple-element.8) | copy-start | bytes 786436

commit v2 on v1

--- a/solution.py
+++ b/solution.py
@@ -20,7 +20,7 @@
 
 
 def gather_kernel(
-    n, banks, m_ref, r_ref, t_ref, s_ref, g_out,
+    n, banks, ends, m_ref, r_ref, t_ref, u_ref, s_ref, g_out,
     x, nar, mx, g, in_sem, own_sem, ls, lr, rs, rr, ms, mr, zs, zr, bs, br,
 ):
     z, b = lax.axis_index("zero"), lax.axis_index("bank")
@@ -29,6 +29,7 @@
     depth = groups * LANES
     chunks = rows // CHUNK
     per = depth // CHUNK
+    body = chunks - ends
 
     def load(e):
         span = pl.ds(e * depth, depth)
@@ -95,6 +96,44 @@
     def own(c):
         return pltpu.make_async_copy(nar.at[span_of(c)], place(c, z), own_sem.at[c])
 
+    def slot(r, o):
+        return u_ref.at[lax.rem(o - jnp.where(r <= 1, 1, 0) + n, n)]
+
+    last = chunks - 1
+
+    def last_leftward(p):
+        src = nar.at[span_of(last)] if p == 0 else slot(z, z + p)
+        return remote(src, slot(z - 1, z + p), ls.at[p, last], lr.at[p, last], "zero", z - 1)
+
+    def last_rightward(p):
+        src = nar.at[span_of(last)] if p == 0 else slot(z, z - p)
+        return remote(src, slot(z + 1, z - p), rs.at[p, last], rr.at[p, last], "zero", z + 1)
+
+    def last_from_right(p):
+        there = slot(z, z + 1 + p)
+        return remote(there, there, ls.at[p, last], lr.at[p, last], "zero", z + 1)
+
+    def last_from_left(p):
+        there = slot(z, z - 1 - p)
+        return remote(there, there, rs.at[p, last], rr.at[p, last], "zero", z - 1)
+
+    def last_own():
+        return pltpu.make_async_copy(nar.at[span_of(last)], slot(z, z), own_sem.at[last])
+
+    inner = (z > 0) & (z < n - 1)
+    goes_left, goes_right = z > 1, z < n - 2
+
+    def send_last():
+        @pl.when(goes_left)
+        def _():
+            last_leftward(0).start()
+
+        @pl.when(goes_right)
+        def _():
+            last_rightward(0).start()
+
+        last_own().start()
+
     def send(c):
         @pl.when(z > 0)
         def _():
@@ -131,31 +170,30 @@
     ]
     for copy in routes:
         copy.start()
-    if experts > 1:
-        maxima(1)
-    for copy in early:
-        copy.wait_recv()
-    each(0, per, narrow)
-    each(0, per, send)
     late = []
     if experts > 1:
-        each(2, experts, maxima)
+        each(1, experts, maxima)
         late = exchange(1, 1, experts)
         for copy in late:
             copy.start()
-        for copy in late:
-            copy.wait_recv()
-        narrow(per)
-
-        def follow(c):
-            narrow(c)
-            send(c - 1)
-
-        each(per + 1, chunks, follow)
+    for copy in early:
+        copy.wait_recv()
+    narrow(0)
+
+    def follow(c):
+        narrow(c)
+        send(c - 1)
+
+    each(1, per, follow)
+    for copy in late:
+        copy.wait_recv()
+    each(per, chunks, follow)
     for copy in routes:
         copy.wait_recv()
-    if experts > 1:
-        send(chunks - 1)
+    if ends:
+        send_last()
+    else:
+        send(last)
     spread = [
         remote(g.at[b], g.at[b], bs.at[k - 1], br.at[k - 1], "bank", lax.rem(b + k, banks)) for k in range(1, banks)
     ]
@@ -182,22 +220,99 @@
                 def _():
                     rightward(p, c).start()
 
-        each(0, chunks, relay)
+        each(0, body, relay)
+        if ends:
+            @pl.when(inner & (z + p <= n - 1))
+            def _():
+                last_from_right(p - 1).wait_recv()
+
+            if p < n - 1:
+                @pl.when(goes_left & (z < n - 1) & (z + p <= n - 1))
+                def _():
+                    last_leftward(p).start()
+
+            @pl.when(inner & (z - p >= 0))
+            def _():
+                last_from_left(p - 1).wait_recv()
+
+            if p < n - 1:
+                @pl.when(goes_right & (z > 0) & (z - p >= 0))
+                def _():
+                    last_rightward(p).start()
 
     for copy in spread:
         copy.wait_recv()
     g_out[...] = g[...]
     for copy in early + late + routes + spread:
         copy.wait_send()
-    each(0, chunks, lambda c: own(c).wait())
+    each(0, body, lambda c: own(c).wait())
+    if ends:
+        last_own().wait()
     for p in range(n - 1):
         @pl.when((z > 0) & (z + p <= n - 1))
         def _():
-            each(0, chunks, lambda c: leftward(p, c).wait_send())
+            each(0, body, lambda c: leftward(p, c).wait_send())
 
         @pl.when((z < n - 1) & (z - p >= 0))
         def _():
-            each(0, chunks, lambda c: rightward(p, c).wait_send())
+            each(0, body, lambda c: rightward(p, c).wait_send())
+
+        if ends:
+            @pl.when(goes_left & (z + p <= n - 1))
+            def _():
+                last_leftward(p).wait_send()
+
+            @pl.when(goes_right & (z - p >= 0))
+            def _():
+                last_rightward(p).wait_send()
+
+
+def copy_kernel(t_ref, o_ref):
+    o_ref[...] = t_ref[...]
+
+
+def last_kernel(slots, info, a_ref, u_ref, _, o_ref):
+    take = (info[1] == 1) & (pl.program_id(0) < slots)
+
+    @pl.when(take)
+    def _():
+        o_ref[...] = a_ref[0]
+
+    @pl.when(jnp.logical_not(take))
+    def _():
+        o_ref[...] = u_ref[0]
+
+
+def finish(n, body, rows, w, gathered, held):
+    whole = jax.ShapeDtypeStruct((rows, n * w), jnp.bfloat16)
+    arrived = lax.ppermute(held[:n - 1], "zero", ((1, 0), (n - 2, n - 1)))
+    most = pl.pallas_call(
+        copy_kernel,
+        grid=(body,),
+        out_shape=whole,
+        in_specs=[pl.BlockSpec((CHUNK, n * w), lambda i: (i, 0))],
+        out_specs=pl.BlockSpec((CHUNK, n * w), lambda i: (i, 0)),
+        cost_estimate=pl.CostEstimate(flops=0, bytes_accessed=4 * body * CHUNK * n * w, transcendentals=0),
+        name="most",
+    )(gathered)
+    z = lax.axis_index("zero")
+    info = jnp.stack([jnp.where(z <= 1, 1, 0), jnp.where((z == 0) | (z == n - 1), 1, 0)]).astype(jnp.int32)
+    return pl.pallas_call(
+        functools.partial(last_kernel, n - 1),
+        grid_spec=pltpu.PrefetchScalarGridSpec(
+            num_scalar_prefetch=1,
+            grid=(n,),
+            in_specs=[
+                pl.BlockSpec((1, CHUNK, w), lambda k, info: (jnp.minimum(k, n - 2), 0, 0)),
+                pl.BlockSpec((1, CHUNK, w), lambda k, info: (k, 0, 0)),
+                pl.BlockSpec(memory_space=pl.ANY),
+            ],
+            out_specs=pl.BlockSpec((CHUNK, w), lambda k, info: (body, lax.rem(k + info[0], n))),
+        ),
+        out_shape=whole,
+        input_output_aliases={3: 0},
+        name="last",
+    )(info, arrived, held, most)
 
 
 def per_device(n, banks, master_down, router_weight, router_gain):
@@ -206,17 +321,21 @@
     rows = experts * depth
     chunks = rows // CHUNK
     groups = depth // LANES
+    ends = 1 if n > 3 else 0
+    body = chunks - ends
     part_router = (router_weight * router_gain[:, None]).astype(jnp.bfloat16).T
     dma = pltpu.SemaphoreType.DMA
-    gathered, scale, routed = pl.pallas_call(
-        functools.partial(gather_kernel, n, banks),
+    gathered, held, scale, routed = pl.pallas_call(
+        functools.partial(gather_kernel, n, banks, ends),
         out_shape=(
-            jax.ShapeDtypeStruct((rows, n * w), jnp.bfloat16),
+            jax.ShapeDtypeStruct((body * CHUNK, n * w), jnp.bfloat16),
+            jax.ShapeDtypeStruct((n, CHUNK, w), jnp.bfloat16),
             jax.ShapeDtypeStruct((experts, groups, LANES), jnp.float32),
             jax.ShapeDtypeStruct((banks, n, few, part), jnp.bfloat16),
         ),
         in_specs=[pl.BlockSpec(memory_space=pl.ANY), pl.BlockSpec(memory_space=pltpu.VMEM)],
         out_specs=(
+            pl.BlockSpec(memory_space=pl.ANY),
             pl.BlockSpec(memory_space=pl.ANY),
             pl.BlockSpec(memory_space=pltpu.VMEM),
             pl.BlockSpec(memory_space=pltpu.VMEM),
@@ -242,6 +361,8 @@
         compiler_params=pltpu.CompilerParams(collective_id=0, has_side_effects=True),
         name="gather",
     )(master_down.reshape(rows, w), part_router)
+    if ends:
+        gathered = finish(n, body, rows, w, gathered, held)
     serve_router = routed.transpose(1, 3, 0, 2).reshape(n * part, banks * few)
     return (
         gathered.reshape(experts, depth, n * w),

time: 585 us -> 573 us (0.979)
  local copies, waits for them, and re-layouts: 25 us -> 4.76 us
  waiting for transfers between devices: 0 us -> 8.18 us
    unnamed x5 -> x6, local copies, waits for them, and re-layouts: 25 us -> 3.25 us
    ppermute x0 -> x1, waiting for transfers between devices: none -> 8.18 us  [finish(): arrived = lax.ppermute(held[:n - 1], 'zero', ((1, 0), (n - 2, n - 1)))]
    pallas_call x1 -> x3, Pallas kernels: 558 us -> 556 us  [the longest x1 525 us: per_device(): pl.pallas_call(functools.partial(gather_kernel, n, banks, ends), out_shap...]
  transfers between devices with their start and end apart: 0 -> 1, of which waited for: 0 -> 1; matrix products, arithmetic and copies ran while one was open for 0% -> 0% of each run, Pallas kernels for 0% -> 5%
where the time goes in v2:
time: 573 us
  Pallas kernels  556 us (97%)
  waiting for transfers between devices  8.18 us (1%)
    pallas_call x1, Pallas kernels, per_device(): pl.pallas_call(functools.partial(gather_kernel, n, banks, ends), out_shap...  525 us
    pallas_call x1, Pallas kernels, finish(): pl.pallas_call(copy_kernel, grid=(body,), out_shape=whole, in_specs=[pl.B...  26.5 us
  transfers between devices with their start and end apart: 1, of which 1 were waited for; matrix products, arithmetic and copies ran while one was open for 0% of the time, Pallas kernels for 5%

profile of v2, /device:TPU:0, one launch (start us, length us, event | category | flops | bytes accessed | tf_op | source)
XLA Modules:
  0.0 572.7 jit_solution(10925228700904051662)
XLA Ops:
  0.6 1.3 fusion.r_ref
  2.0 524.7 %gather.1 = (bf16[7680,2048]{1,0:T(8,128)(2,1)}, bf16[4,512,512]{2,1,0:T(8,128)(2,1)}, f32[8,8,128]{2,1,0:T(8,128)}, bf16[8,4,8,512]{3,2,1,0:T(8,128)(2,1)}) custom-call(f32[8192,512]{1,0:T(8,128)} %bitcast.14, bf16[8,512]{1,0:T(8,128)(2,1)} %fusion.r_ref), custom_call_target="tpu_custom_call" | custom-call | tf_op jit(solution)/shard_map/gather/pallas_call | solution.py:328
  526.7 1.5 slice.3
  528.2 1.3 collective-permute-start
  529.5 1.4 copy.9
  530.9 26.5 %most.1._ = bf16[8192,2048]{1,0:T(8,128)(2,1)} custom-call(bf16[7680,2048]{1,0:T(8,128)(2,1)} %get-tuple-element.8.t_ref), custom_call_target="tpu_custom_call" | custom-call | bytes 62914560 | tf_op jit(solution)/shard_map/most/pallas_call | solution.py:289
  557.4 0.6 pad_add_fusion.info
  558.0 0.0 copy-start.1
  558.0 8.2 %collective-permute-done.a_ref = bf16[3,512,512]{2,1,0:T(8,128)(2,1)S(1)} collective-permute-done((bf16[3,512,512]{2,1,0:T(8,128)(2,1)S(1)}, bf16[3,512,512]{2,1,0:T(8,128)(2,1)S(1)}, u32[]{:S(2)}, u32[]{:S(2)}) %collective-permute-start) | collective-permute-done | bytes 1572896 | tf_op jit(solution)/shard_map/ppermute | solution.py:288
  566.2 0.0 copy-start
  566.2 1.2 copy-done
  567.3 4.7 last.1
  572.0 0.0 copy-done.1
  572.0 0.7 copy.12
Async XLA Ops:
  528.2 38.0 %collective-permute-start = (bf16[3,512,512]{2,1,0:T(8,128)(2,1)S(1)}, bf16[3,512,512]{2,1,0:T(8,128)(2,1)S(1)}, u32[]{:S(2)}, u32[]{:S(2)}) collective-permute-start(bf16[3,512,512]{2,1,0:T(8,128)(2,1)S(1)} %slice.3), channel_id=1, source_target_pairs={{1,0},{2,3},{5,4},{6,7},{9,8},{10,11},{13,12},{14,15},{17,16},{18,... | collective-permute-start | bytes 4718600 | tf_op jit(solution)/shard_map/ppermute | solution.py:288
  558.0 14.0 %copy-start.1 = (bf16[8,4,8,512]{3,2,1,0:T(8,128)(2,1)S(1)}, bf16[8,4,8,512]{3,2,1,0:T(8,128)(2,1)}, u32[]{:S(2)}) copy-start(bf16[8,4,8,512]{3,2,1,0:T(8,128)(2,1)} %get-tuple-element.10) | copy-start | bytes 786436
  566.2 1.2 copy-start
